TPU v7x, 256 devices: a whole 4x4x8 slice. The times are simulated.
256 devices in a mesh: dp: 64 (over z, x, core), outer: 4 (over y).
Axes of the slice: x: 4, y: 4, z: 8, core: 2. Of those that a mesh axis runs over, the one named last changes fastest.
Arguments:
- partials: bfloat16 [4, 64, 2, 128, 8192], P('outer', 'dp'), may hold values from -3500 to 3500, as said below
- master: float32 [2, 128, 8192], P(None, 'dp'), may hold values from -6 to 6
- m_codes: bfloat16 [2, 128, 8192], P(None, 'dp'), may hold values from -1 to 1
- v_codes: bfloat16 [2, 128, 8192], P(None, 'dp'), may hold values from 0.049804688 to 1
- m_scales: float32 [2, 128, 4], P(None, 'dp'), may hold values from 0.0001 to 0.001
- v_scales: float32 [2, 128, 4], P(None, 'dp'), may hold values from 1e-08 to 1e-07
Outputs:
- new_master: float32 [2, 128, 8192], P(None, 'dp')
- new_m_codes: bfloat16 [2, 128, 8192], P(None, 'dp')
- new_v_codes: bfloat16 [2, 128, 8192], P(None, 'dp')
- new_m_scales: float32 [2, 128, 4], P(None, 'dp')
- new_v_scales: float32 [2, 128, 4], P(None, 'dp')
- weights: bfloat16 [2, 128, 8192], replicated
Inputs may be any that keep to these rules, and one draw needn't show every extreme that they name: Gradient partials of real values; entries vary from row to row and column to column.
All inputs are finite; a program needn't handle non-finite values. Where the computation divides by a largest or mean magnitude, that divisor is 1e-20 or more.
Results may differ from a plain program's by a relative error of at most 0.0004.
Values may be sent and summed in bfloat16 or wider, within the bound.
A program may use at most 64 MiB of HBM per device.

v0:
```python
import functools
import jax
import jax.numpy as jnp
from jax import lax
from jax.sharding import Mesh
from jax.sharding import PartitionSpec as P

BLOCK = 2048
STEP = 10
DP = ("dp_0", "dp_1", "dp_2")
DP_OUTER = ("dp_0", "dp_1", "dp_2", "outer")


def cut_along(x, dim, count):
    lengths = x.shape
    pieces = x.reshape(*lengths[:dim], count, lengths[dim] // count, *lengths[dim + 1 :])
    return jnp.moveaxis(pieces, dim, 0)


def sum_at_owner(x, axis, dim):
    pieces = cut_along(x, dim, lax.axis_size(axis))
    arrived = lax.all_to_all(pieces, axis, split_axis=0, concat_axis=0, tiled=True)
    return arrived.sum(axis=0)


def over_axes(x, axes):
    return functools.reduce(lax.psum, axes, x)


def sent_together(arrays, axis, dim, along):
    widths = [a.shape[along] for a in arrays]
    both = jnp.concatenate(arrays, axis=along)
    result = lax.all_gather(both, axis, axis=dim, tiled=True)
    return tuple(jnp.split(result, [sum(widths[:k]) for k in range(1, len(widths))], axis=along))


def in_order(pieces, dim):
    lengths = list(pieces.shape[1:])
    lengths[dim] *= pieces.shape[0]
    return jnp.moveaxis(pieces, 0, dim).reshape(lengths)


def gather_in_order(x, axes, order):
    pieces = x[None]
    for k in order:
        pieces = lax.all_gather(pieces, axes[k], axis=0, tiled=True)
    block = [lax.axis_size(axes[k]) for k in reversed(order)]
    pieces = pieces.reshape(*block, *x.shape)
    turned = sorted(range(len(order)), key=lambda place: order[len(order) - 1 - place])
    return pieces.transpose(*turned, *range(len(order), pieces.ndim)).reshape(-1, *x.shape)


def whole_of(x, axes, order, dim):
    return in_order(gather_in_order(x, axes, order), dim)


def adam_blocks(gradient, master, m_codes, v_codes, m_scales, v_scales, clip_factor):
    count = gradient.shape[0]
    rows = gradient.shape[1]
    blocks = gradient.shape[2] // BLOCK
    shape_four = (count, rows, blocks, BLOCK)
    moment = m_codes.astype(jnp.float32).reshape(shape_four) * m_scales[..., None]
    second = v_codes.astype(jnp.float32).reshape(shape_four) * v_scales[..., None]
    scaled = clip_factor * gradient.reshape(shape_four)
    moment = 0.9 * moment + 0.1 * scaled
    second = 0.95 * second + 0.05 * scaled * scaled
    update = moment / (1.0 - 0.9**STEP) / (jnp.sqrt(second / (1.0 - 0.95**STEP)) + 1e-08)
    fresh = master - 0.01 * update.reshape(master.shape)
    m_top = jnp.max(jnp.abs(moment), axis=3) + 1e-20
    v_top = jnp.max(jnp.abs(second), axis=3) + 1e-20
    m_next = (moment / m_top[..., None]).astype(jnp.bfloat16).reshape(master.shape)
    v_next = (second / v_top[..., None]).astype(jnp.bfloat16).reshape(master.shape)
    return (fresh, m_next, v_next, m_top, v_top, fresh.astype(jnp.bfloat16))


def body(partials, master, m_codes, v_codes, m_scales, v_scales):
    own_terms = partials[0, 0]
    received = lax.all_to_all(own_terms[None], "outer", split_axis=3, concat_axis=0, tiled=True)
    column_part = jnp.sum(received.astype(jnp.float32), axis=0)
    gradient = sum_at_owner(column_part, DP, 1)
    total = over_axes(jnp.sum(gradient * gradient), DP_OUTER)
    clip_factor = 1.0 / jnp.maximum(jnp.sqrt(total), 1.0)
    quarter = gradient.shape[2]
    offset = lax.axis_index("outer") * quarter
    scale_count = quarter // BLOCK
    scale_offset = lax.axis_index("outer") * scale_count
    results = adam_blocks(
        gradient,
        lax.dynamic_slice_in_dim(master, offset, quarter, 2),
        lax.dynamic_slice_in_dim(m_codes, offset, quarter, 2),
        lax.dynamic_slice_in_dim(v_codes, offset, quarter, 2),
        lax.dynamic_slice_in_dim(m_scales, scale_offset, scale_count, 2),
        lax.dynamic_slice_in_dim(v_scales, scale_offset, scale_count, 2),
        clip_factor,
    )
    fresh, m_next, v_next, m_top, v_top, rounded = results
    fresh, m_top, v_top = (
        lax.all_gather(fresh, "outer", axis=2, tiled=True),
        *sent_together((m_top, v_top), "outer", 2, 0),
    )
    m_next, v_next, rounded = sent_together((m_next, v_next, rounded), "outer", 2, 0)
    weights = whole_of(rounded, DP, (1, 0, 2), 1)
    return (fresh, m_next, v_next, m_top, v_top, weights)


def solution(mesh):
    finer = Mesh(
        mesh.devices.reshape(8, 4, 2, mesh.shape["outer"]), ("dp_0", "dp_1", "dp_2", "outer")
    )
    placed = (
        P("outer", DP, None, None, None),
        P(None, DP, None),
        P(None, DP, None),
        P(None, DP, None),
        P(None, DP, None),
        P(None, DP, None),
    )
    return jax.shard_map(
        body,
        mesh=finer,
        in_specs=placed,
        out_specs=(
            P(None, DP, None),
            P(None, DP, None),
            P(None, DP, None),
            P(None, DP, None),
            P(None, DP, None),
            P(),
        ),
        check_vma=False,
    )
```

profile of v0, /device:TPU:2, one launch (start us, length us, event | category | flops | bytes accessed | tf_op | source)
XLA Modules:
  0.0 303.8 jit_solution(3375123823743726198)
XLA Ops:
  7.2 11.2 %copy.36 = bf16[1,1,2,128,8192]{3,2,4,1,0:T(2,128)(2,1)} copy(bf16[1,1,2,128,8192]{4,3,2,1,0:T(8,128)(2,1)} %param.6) | data formatting | bytes 8388608 | tf_op args[0]
  18.3 53.3 %all_to_all.14 = bf16[1,2,128,8192]{2,1,0,3:T(2,128)(2,1)S(1)} all-to-all(bf16[1,2,128,8192]{2,1,0,3:T(2,128)(2,1)} %bitcast.21), channel_id=1, replica_groups=mesh['dp_0'=8,'dp_1'=4,'dp_2'=2,'outer'=4] {'outer'}, dimensions={3} | all-to-all | bytes 8388608 | tf_op jit(solution)/shard_map/all_to_all | solution.py:78
  71.6 5.1 %convert_reduce_fusion = f32[2,128,2048]{1,0,2:T(2,128)S(1)} fusion(bf16[2,128,4,2048]{1,0,3,2:T(2,128)(2,1)S(1)} %bitcast.18), kind=kLoop, calls=%fused_computation | loop fusion | flops 3670016 | bytes 6291456 | tf_op jit(solution)/shard_map/reduce_sum | solution.py:79
  76.7 3.5 %copy.37 = f32[2,128,2048]{2,0,1:T(2,128)} copy(f32[2,128,2048]{1,0,2:T(2,128)S(1)} %convert_reduce_fusion) | data formatting | bytes 4194304 | tf_op jit(solution)/shard_map/reduce_sum | solution.py:79
  80.2 0.0 copy-start
  80.2 0.0 copy-start.1
  80.2 4.9 %copy.38 = f32[64,2,2,2048]{3,2,1,0:T(2,128)} copy(f32[64,2,2,2048]{3,1,2,0:T(2,128)} %bitcast.22) | data formatting | bytes 4194304 | tf_op jit(solution)/shard_map/transpose | solution.py:17
  85.1 12.0 %all-to-all-start.1 = ((f32[64,2,2,2048]{3,2,1,0:T(2,128)}), f32[64,2,2,2048]{3,2,1,0:T(2,128)S(1)}, u32[]{:S(2)}, u32[]{:S(2)}) async-start(f32[64,2,2,2048]{3,2,1,0:T(2,128)} %copy.38), calls=%async_computation.1 | async-start | bytes 4194304 | tf_op jit(solution)/shard_map/all_to_all | solution.py:22
  97.1 0.0 all-gather.4.cloned.1.call-start
  97.2 0.0 copy-done
  97.2 0.0 copy-done.1
  97.2 0.2 dynamic-slice_reduce_fusion
  97.4 51.0 %all-to-all-done.1 = f32[64,2,2,2048]{3,2,1,0:T(2,128)S(1)} async-done(((f32[64,2,2,2048]{3,2,1,0:T(2,128)}), f32[64,2,2,2048]{3,2,1,0:T(2,128)S(1)}, u32[]{:S(2)}, u32[]{:S(2)}) %all-to-all-start.1) | async-done | bytes 2097184 | tf_op jit(solution)/shard_map/all_to_all | solution.py:22
  148.4 0.8 reduce_sum.28
  149.2 0.6 multiply_reduce_fusion
  149.8 15.4 %psum.28 = f32[]{:T(128)} all-reduce(f32[]{:T(128)} %multiply_reduce_fusion), channel_id=1, replica_groups=mesh['dp_0'=8,'dp_1'=4,'dp_2'=2,'outer'=4] {'dp_0'}, use_global_device_ids=true, to_apply=%region_3.0 | all-reduce | flops 1 | bytes 8 | tf_op jit(solution)/shard_map/psum | solution.py:27
  165.2 9.2 %psum.29 = f32[]{:T(128)} all-reduce(f32[]{:T(128)} %psum.28), channel_id=1, replica_groups=mesh['dp_0'=8,'dp_1'=4,'dp_2'=2,'outer'=4] {'dp_1'}, use_global_device_ids=true, to_apply=%region_4.0 | all-reduce | flops 1 | bytes 8 | tf_op jit(solution)/shard_map/psum | solution.py:27
  174.4 3.1 %psum.30 = f32[]{:T(128)} all-reduce(f32[]{:T(128)} %psum.29), channel_id=1, replica_groups=mesh['dp_0'=8,'dp_1'=4,'dp_2'=2,'outer'=4] {'dp_2'}, use_global_device_ids=true, to_apply=%region_5.0 | all-reduce | flops 1 | bytes 8 | tf_op jit(solution)/shard_map/psum | solution.py:27
  177.5 9.5 %psum.31 = f32[]{:T(128)} all-reduce(f32[]{:T(128)} %psum.30), channel_id=1, replica_groups=mesh['dp_0'=8,'dp_1'=4,'dp_2'=2,'outer'=4] {'outer'}, use_global_device_ids=true, to_apply=%region_6.0 | all-reduce | flops 1 | bytes 8 | tf_op jit(solution)/shard_map/psum | solution.py:27
  187.7 1.0 abs_reduce_fusion.1
  188.7 0.9 fusion.4
  189.6 0.1 pad_maximum_fusion
  189.6 12.1 %all_gather.19 = bf16[6,2,8192]{2,1,0:T(2,128)(2,1)S(1)} all-gather(bf16[6,2,2048]{2,1,0:T(2,128)(2,1)S(1)} %pad_maximum_fusion), channel_id=1, replica_groups=mesh['dp_0'=8,'dp_1'=4,'dp_2'=2,'outer'=4] {'outer'}, dimensions={2}, use_global_device_ids=true | all-gather | bytes 245760 | tf_op jit(solution)/shard_map/all_gather | solution.py:33
  201.8 0.8 fusion.5
  202.6 12.4 %all-gather = bf16[8,2,8192]{2,1,0:T(2,128)(2,1)} all-gather(bf16[2,2,8192]{2,1,0:T(2,128)(2,1)S(1)} %get-tuple-element.48), channel_id=2, replica_groups=mesh['dp_0'=8,'dp_1'=4,'dp_2'=2,'outer'=4] {'dp_1'}, dimensions={0}, use_global_device_ids=true | all-gather | bytes 327680 | tf_op jit(solution)/shard_map/all_gather | solution.py:46
  214.9 0.0 all-gather.4.cloned.1.call-update
  214.9 0.0 all-gather.6.cloned.1.call-start
  215.0 38.6 %all-gather.4.cloned.1.call-done = bf16[32,2,2,8192]{3,2,1,0:T(2,128)(2,1)} async-done(((bf16[4,2,2,8192]{3,2,1,0:T(2,128)(2,1)}), bf16[32,2,2,8192]{3,2,1,0:T(2,128)(2,1)}) %all-gather.4.cloned.1.call-update) | async-done | bytes 2097168 | tf_op jit(solution)/shard_map/all_gather | solution.py:46
  253.5 0.0 all-gather.6.cloned.1.call-update
  253.6 0.1 copy.39
  253.7 9.7 %all_gather.20 = f32[4,2,4]{0,1,2:T(2,128)S(1)} all-gather(f32[4,2,1]{0,1,2:T(2,128)S(1)} %copy.39), channel_id=1, replica_groups=mesh['dp_0'=8,'dp_1'=4,'dp_2'=2,'outer'=4] {'outer'}, dimensions={2}, use_global_device_ids=true | all-gather | bytes 160 | tf_op jit(solution)/shard_map/all_gather | solution.py:33
  263.4 12.2 %all_gather.18 = f32[2,2,8192]{2,1,0:T(2,128)S(1)} all-gather(f32[2,2,2048]{2,1,0:T(2,128)S(1)} %get-tuple-element.47), channel_id=1, replica_groups=mesh['dp_0'=8,'dp_1'=4,'dp_2'=2,'outer'=4] {'outer'}, dimensions={2}, use_global_device_ids=true | all-gather | bytes 163840 | tf_op jit(solution)/shard_map/all_gather | solution.py:98
  275.6 0.1 fusion.6
  275.6 0.7 copy.42
  276.3 0.7 copy.43
  277.0 0.0 all-gather.6.cloned.1.call-done
  277.0 6.1 %copy.40 = bf16[2,8,4,2,2,8192]{5,4,3,0,2,1:T(2,128)(2,1)S(1)} copy(bf16[2,8,4,2,2,8192]{5,4,3,2,1,0:T(2,128)(2,1)} %bitcast.23) | data formatting | bytes 8388608 | tf_op jit(solution)/shard_map/reshape | solution.py:48
  283.1 6.3 %copy.41 = bf16[2,64,2,8192]{3,0,2,1:T(2,128)(2,1)} copy(bf16[2,64,2,8192]{3,2,0,1:T(2,128)(2,1)S(1)} %bitcast.19) | data formatting | bytes 8388608 | tf_op jit(solution)/shard_map/transpose | solution.py:40
  289.4 6.9 %copy.44 = bf16[2,128,8192]{2,1,0:T(8,128)(2,1)} copy(bf16[2,128,8192]{2,0,1:T(2,128)(2,1)} %bitcast.20) | data formatting | bytes 8388608
  296.3 0.7 copy.46
  (3 shorter events, 0.0 us)
Async XLA Ops:
  80.2 17.0 %copy-start = (f32[2,2,4]{2,1,0:T(2,128)S(1)}, f32[2,2,4]{2,1,0:T(2,128)}, u32[]{:S(2)}) copy-start(f32[2,2,4]{2,1,0:T(2,128)} %param.11) | copy-start | bytes 196
  80.2 17.0 %copy-start.1 = (f32[2,2,4]{2,1,0:T(2,128)S(1)}, f32[2,2,4]{2,1,0:T(2,128)}, u32[]{:S(2)}) copy-start(f32[2,2,4]{2,1,0:T(2,128)} %param.10) | copy-start | bytes 196
  85.1 63.3 %all-to-all-start.1 = ((f32[64,2,2,2048]{3,2,1,0:T(2,128)}), f32[64,2,2,2048]{3,2,1,0:T(2,128)S(1)}, u32[]{:S(2)}, u32[]{:S(2)}) async-start(f32[64,2,2,2048]{3,2,1,0:T(2,128)} %copy.38), calls=%async_computation.1 | async-start | bytes 4194304 | tf_op jit(solution)/shard_map/all_to_all | solution.py:22
  97.1 156.4 %all-gather.4.cloned.1.call-start = ((), (), s32[]{:S(2)}) async-start(), calls=%async_computation.2 | async-start | bytes 2359296 | tf_op jit(solution)/shard_map/all_gather | solution.py:46
  214.9 62.0 %all-gather.6.cloned.1.call-start = ((), (), s32[]{:S(2)}) async-start(), calls=%async_computation.3 | async-start | bytes 6291456 | tf_op jit(solution)/shard_map/all_gather | solution.py:46
Sparse Core Ops, SparseCore 0:
  215.1 38.4 all-gather.3
  255.3 17.5 all-gather.5
where the time goes:
time: 305 us; the launch traced here: 304 us
  blocking collectives  137 us (45%)
  waiting for transfers between devices  89.6 us (29%)
  local copies, waits for them, and re-layouts  42 us (14%)
  between operations  14.8 us (5%)
  starting transfers between devices  12.1 us (4%)
  other arithmetic  8.43 us (3%)
    all_to_all x1, blocking collectives, body(): lax.all_to_all(own_terms[None], 'outer', split_axis=3, concat_axis=0, til...  53.3 us
    all_to_all x1, waiting for transfers between devices, sum_at_owner(): lax.all_to_all(pieces, axis, split_axis=0, concat_axis=0, tiled=True)  51 us
    all_gather x2, waiting for transfers between devices, gather_in_order(): pieces = lax.all_gather(pieces, axes[k], axis=0, tiled=True)  38.6 us
    psum x4, blocking collectives, over_axes(): return functools.reduce(lax.psum, axes, x)  37.2 us
    all_gather x2, blocking collectives, sent_together(): result = lax.all_gather(both, axis, axis=dim, tiled=True)  21.8 us
    unnamed x9, local copies, waits for them, and re-layouts  20 us
    all_gather x1, blocking collectives, gather_in_order(): pieces = lax.all_gather(pieces, axes[k], axis=0, tiled=True)  12.4 us
    all_gather x1, blocking collectives, body(): lax.all_gather(fresh, 'outer', axis=2, tiled=True)  12.2 us
  transfers between devices with their start and end apart: 3, of which 2 were waited for; matrix products, arithmetic and copies ran while one was open for 1% of the time, Pallas kernels for 0%

commit v1 on v0

--- a/solution.py
+++ b/solution.py
@@ -75,7 +75,12 @@
 
 def body(partials, master, m_codes, v_codes, m_scales, v_scales):
     own_terms = partials[0, 0]
-    received = lax.all_to_all(own_terms[None], "outer", split_axis=3, concat_axis=0, tiled=True)
+    received = jnp.concatenate(
+        lax.all_to_all(
+            jnp.stack(jnp.split(own_terms[None], lax.axis_size("outer"), axis=3)), "outer", 0, 0
+        ),
+        axis=0,
+    )
     column_part = jnp.sum(received.astype(jnp.float32), axis=0)
     gradient = sum_at_owner(column_part, DP, 1)
     total = over_axes(jnp.sum(gradient * gradient), DP_OUTER)

time: 305 us -> 288 us (0.944)
  local copies, waits for them, and re-layouts: 42 us -> 30 us
  other arithmetic: 8.43 us -> 4.71 us
    unnamed x9 -> x8, local copies, waits for them, and re-layouts: 20 us -> 8.89 us
    reduce_sum x1, other arithmetic: 5.08 us -> 0.79 us  [body(): column_part = jnp.sum(received.astype(jnp.float32), axis=0)]
where the time goes in v1:
time: 288 us
  blocking collectives  137 us (48%)
  waiting for transfers between devices  89.6 us (31%)
  local copies, waits for them, and re-layouts  30 us (10%)
  between operations  14.9 us (5%)
  starting transfers between devices  12.1 us (4%)
  other arithmetic  4.71 us (2%)
    all_to_all x1, blocking collectives, body(): lax.all_to_all(jnp.stack(jnp.split(own_terms[None], lax.axis_size('outer'...  53.1 us
    all_to_all x1, waiting for transfers between devices, sum_at_owner(): lax.all_to_all(pieces, axis, split_axis=0, concat_axis=0, tiled=True)  51 us
    all_gather x2, waiting for transfers between devices, gather_in_order(): pieces = lax.all_gather(pieces, axes[k], axis=0, tiled=True)  38.6 us
    psum x4, blocking collectives, over_axes(): return functools.reduce(lax.psum, axes, x)  37.2 us
    all_gather x2, blocking collectives, sent_together(): result = lax.all_gather(both, axis, axis=dim, tiled=True)  21.8 us
    all_gather x1, blocking collectives, gather_in_order(): pieces = lax.all_gather(pieces, axes[k], axis=0, tiled=True)  12.4 us
    all_gather x1, blocking collectives, body(): lax.all_gather(fresh, 'outer', axis=2, tiled=True)  12.2 us
    all_to_all x1, starting transfers between devices, sum_at_owner(): lax.all_to_all(pieces, axis, split_axis=0, concat_axis=0, tiled=True)  12 us
  transfers between devices with their start and end apart: 3, of which 2 were waited for; matrix products, arithmetic and copies ran while one was open for 1% of the time, Pallas kernels for 0%

profile of v1, /device:TPU:2, one launch (start us, length us, event | category | flops | bytes accessed | tf_op | source)
XLA Modules:
  0.0 287.9 jit_solution(633560168804519845)
XLA Ops:
  7.2 2.8 slice_bitcast_fusion.3
  9.9 0.6 pad_maximum_fusion
  10.5 53.1 %all_to_all.10 = bf16[4,1,2,128,2048]{4,3,2,1,0:T(8,128)(2,1)S(1)} all-to-all(bf16[4,1,2,128,2048]{4,3,2,1,0:T(8,128)(2,1)S(1)} %pad_maximum_fusion), channel_id=1, replica_groups=mesh['dp_0'=8,'dp_1'=4,'dp_2'=2,'outer'=4] {'outer'}, dimensions={0} | all-to-all | bytes 8388608 | tf_op jit(solution)/shard_map/all_to_all | solution.py:79
  63.6 0.8 convert_reduce_fusion
  64.4 1.6 copy.33
  66.0 0.0 copy-start
  66.0 0.0 copy-start.1
  66.0 3.2 %copy.34 = f32[64,2,2,2048]{3,2,1,0:T(2,128)} copy(f32[64,2,2,2048]{3,1,2,0:T(2,128)S(1)} %bitcast.26) | data formatting | bytes 4194304 | tf_op jit(solution)/shard_map/transpose | solution.py:17
  69.2 12.0 %all-to-all-start.1 = ((f32[64,2,2,2048]{3,2,1,0:T(2,128)}), f32[64,2,2,2048]{3,2,1,0:T(2,128)S(1)}, u32[]{:S(2)}, u32[]{:S(2)}) async-start(f32[64,2,2,2048]{3,2,1,0:T(2,128)} %copy.34), calls=%async_computation.1 | async-start | bytes 4194304 | tf_op jit(solution)/shard_map/all_to_all | solution.py:22
  81.3 0.0 all-gather.4.cloned.1.call-start
  81.3 0.0 copy-done
  81.3 0.0 copy-done.1
  81.3 0.2 dynamic-slice_reduce_fusion
  81.5 51.0 %all-to-all-done.1 = f32[64,2,2,2048]{3,2,1,0:T(2,128)S(1)} async-done(((f32[64,2,2,2048]{3,2,1,0:T(2,128)}), f32[64,2,2,2048]{3,2,1,0:T(2,128)S(1)}, u32[]{:S(2)}, u32[]{:S(2)}) %all-to-all-start.1) | async-done | bytes 2097184 | tf_op jit(solution)/shard_map/all_to_all | solution.py:22
  132.5 0.8 reduce_sum.28
  133.3 0.6 multiply_reduce_fusion
  133.9 15.4 %psum.28 = f32[]{:T(128)} all-reduce(f32[]{:T(128)} %multiply_reduce_fusion), channel_id=1, replica_groups=mesh['dp_0'=8,'dp_1'=4,'dp_2'=2,'outer'=4] {'dp_0'}, use_global_device_ids=true, to_apply=%region_3.0 | all-reduce | flops 1 | bytes 8 | tf_op jit(solution)/shard_map/psum | solution.py:27
  149.3 9.2 %psum.29 = f32[]{:T(128)} all-reduce(f32[]{:T(128)} %psum.28), channel_id=1, replica_groups=mesh['dp_0'=8,'dp_1'=4,'dp_2'=2,'outer'=4] {'dp_1'}, use_global_device_ids=true, to_apply=%region_4.0 | all-reduce | flops 1 | bytes 8 | tf_op jit(solution)/shard_map/psum | solution.py:27
  158.5 3.1 %psum.30 = f32[]{:T(128)} all-reduce(f32[]{:T(128)} %psum.29), channel_id=1, replica_groups=mesh['dp_0'=8,'dp_1'=4,'dp_2'=2,'outer'=4] {'dp_2'}, use_global_device_ids=true, to_apply=%region_5.0 | all-reduce | flops 1 | bytes 8 | tf_op jit(solution)/shard_map/psum | solution.py:27
  161.6 9.5 %psum.31 = f32[]{:T(128)} all-reduce(f32[]{:T(128)} %psum.30), channel_id=1, replica_groups=mesh['dp_0'=8,'dp_1'=4,'dp_2'=2,'outer'=4] {'outer'}, use_global_device_ids=true, to_apply=%region_6.0 | all-reduce | flops 1 | bytes 8 | tf_op jit(solution)/shard_map/psum | solution.py:27
  171.9 1.0 abs_reduce_fusion.1
  172.8 0.9 fusion.4
  173.7 0.1 pad_maximum_fusion.1
  173.8 12.1 %all_gather.19 = bf16[6,2,8192]{2,1,0:T(2,128)(2,1)S(1)} all-gather(bf16[6,2,2048]{2,1,0:T(2,128)(2,1)S(1)} %pad_maximum_fusion.1), channel_id=1, replica_groups=mesh['dp_0'=8,'dp_1'=4,'dp_2'=2,'outer'=4] {'outer'}, dimensions={2}, use_global_device_ids=true | all-gather | bytes 245760 | tf_op jit(solution)/shard_map/all_gather | solution.py:33
  185.9 0.8 fusion.5
  186.7 12.4 %all-gather = bf16[8,2,8192]{2,1,0:T(2,128)(2,1)} all-gather(bf16[2,2,8192]{2,1,0:T(2,128)(2,1)S(1)} %get-tuple-element.52), channel_id=2, replica_groups=mesh['dp_0'=8,'dp_1'=4,'dp_2'=2,'outer'=4] {'dp_1'}, dimensions={0}, use_global_device_ids=true | all-gather | bytes 327680 | tf_op jit(solution)/shard_map/all_gather | solution.py:46
  199.0 0.0 all-gather.4.cloned.1.call-update
  199.1 0.0 all-gather.6.cloned.1.call-start
  199.1 38.6 %all-gather.4.cloned.1.call-done = bf16[32,2,2,8192]{3,2,1,0:T(2,128)(2,1)} async-done(((bf16[4,2,2,8192]{3,2,1,0:T(2,128)(2,1)}), bf16[32,2,2,8192]{3,2,1,0:T(2,128)(2,1)}) %all-gather.4.cloned.1.call-update) | async-done | bytes 2097168 | tf_op jit(solution)/shard_map/all_gather | solution.py:46
  237.7 0.0 all-gather.6.cloned.1.call-update
  237.7 0.1 copy.35
  237.8 9.7 %all_gather.20 = f32[4,2,4]{0,1,2:T(2,128)S(1)} all-gather(f32[4,2,1]{0,1,2:T(2,128)S(1)} %copy.35), channel_id=1, replica_groups=mesh['dp_0'=8,'dp_1'=4,'dp_2'=2,'outer'=4] {'outer'}, dimensions={2}, use_global_device_ids=true | all-gather | bytes 160 | tf_op jit(solution)/shard_map/all_gather | solution.py:33
  247.5 0.1 fusion.6
  247.6 0.7 copy.38
  248.3 0.7 copy.39
  248.9 12.2 %all_gather.18 = f32[2,2,8192]{2,1,0:T(2,128)S(1)} all-gather(f32[2,2,2048]{2,1,0:T(2,128)S(1)} %get-tuple-element.47), channel_id=1, replica_groups=mesh['dp_0'=8,'dp_1'=4,'dp_2'=2,'outer'=4] {'outer'}, dimensions={2}, use_global_device_ids=true | all-gather | bytes 163840 | tf_op jit(solution)/shard_map/all_gather | solution.py:103
  261.1 0.0 all-gather.6.cloned.1.call-done
  261.1 6.1 %copy.36 = bf16[2,8,4,2,2,8192]{5,4,3,0,2,1:T(2,128)(2,1)S(1)} copy(bf16[2,8,4,2,2,8192]{5,4,3,2,1,0:T(2,128)(2,1)} %bitcast.28) | data formatting | bytes 8388608 | tf_op jit(solution)/shard_map/reshape | solution.py:48
  267.2 6.3 %copy.37 = bf16[2,64,2,8192]{3,0,2,1:T(2,128)(2,1)} copy(bf16[2,64,2,8192]{3,2,0,1:T(2,128)(2,1)S(1)} %bitcast.24) | data formatting | bytes 8388608 | tf_op jit(solution)/shard_map/transpose | solution.py:40
  273.5 6.9 %copy.40 = bf16[2,128,8192]{2,1,0:T(8,128)(2,1)} copy(bf16[2,128,8192]{2,0,1:T(2,128)(2,1)} %bitcast.25) | data formatting | bytes 8388608
  280.4 0.7 copy.42
  (3 shorter events, 0.0 us)
Async XLA Ops:
  66.0 15.3 %copy-start = (f32[2,2,4]{2,1,0:T(2,128)S(1)}, f32[2,2,4]{2,1,0:T(2,128)}, u32[]{:S(2)}) copy-start(f32[2,2,4]{2,1,0:T(2,128)} %param.11) | copy-start | bytes 196
  66.0 15.3 %copy-start.1 = (f32[2,2,4]{2,1,0:T(2,128)S(1)}, f32[2,2,4]{2,1,0:T(2,128)}, u32[]{:S(2)}) copy-start(f32[2,2,4]{2,1,0:T(2,128)} %param.10) | copy-start | bytes 196
  69.2 63.3 %all-to-all-start.1 = ((f32[64,2,2,2048]{3,2,1,0:T(2,128)}), f32[64,2,2,2048]{3,2,1,0:T(2,128)S(1)}, u32[]{:S(2)}, u32[]{:S(2)}) async-start(f32[64,2,2,2048]{3,2,1,0:T(2,128)} %copy.34), calls=%async_computation.1 | async-start | bytes 4194304 | tf_op jit(solution)/shard_map/all_to_all | solution.py:22
  81.3 156.4 %all-gather.4.cloned.1.call-start = ((), (), s32[]{:S(2)}) async-start(), calls=%async_computation.2 | async-start | bytes 2359296 | tf_op jit(solution)/shard_map/all_gather | solution.py:46
  199.1 62.0 %all-gather.6.cloned.1.call-start = ((), (), s32[]{:S(2)}) async-start(), calls=%async_computation.3 | async-start | bytes 6291456 | tf_op jit(solution)/shard_map/all_gather | solution.py:46
Sparse Core Ops, SparseCore 0:
  199.2 38.4 all-gather.3
  239.5 17.5 all-gather.5
